TPU v7x, 32 devices: a whole 2x2x4 slice. The times are simulated.
32 devices in a mesh: dp: 8 (over y, x, core), vocab: 4 (over z).
Axes of the slice: x: 2, y: 2, z: 4, core: 2. Of those that a mesh axis runs over, the one named last changes fastest.
Arguments:
- hidden: float32 [16, 4608], P('dp'), may hold values from -6 to 6
- norm_gain: float32 [4608], replicated, may hold values from 0.5 to 1.5
- embed_table: bfloat16 [12288, 4608], P(('dp', 'vocab')), as said below
- tokens: int32 [16, 3], replicated, may hold values from 0 to 12287, as said below
Outputs:
- log_probs: float32 [16, 3], P('dp')
- final_hidden: float32 [16, 4608], P('dp')
Inputs may be any that keep to these rules, and one draw needn't show every extreme that they name: `tokens`: token ids are vocabulary entries. `embed_table`: entries lie between -21 / sqrt(4608) and 21 / sqrt(4608).
All inputs are finite; a program needn't handle non-finite values.
Results may differ from a plain program's by a relative error of at most 0.0003.
Values may be sent and summed in bfloat16 or wider, within the bound.
A program may use at most 64 MiB of HBM per device.

v0:
```python
import math

import jax
import jax.numpy as jnp
from jax import lax
from jax.sharding import PartitionSpec as P

D = 4608
STEPS = 3


epsilon_value = 1e-06
softcap_value = 30.0


def project_rows(normed, embed_table):
    return lax.dot_general(
        normed, embed_table, (((1,), (1,)), ((), ())), preferred_element_type=jnp.float32
    )


def on_device(hidden, norm_gain, embed_table, tokens):
    own_rows = hidden.shape[0]
    shard_rows = embed_table.shape[0]
    own_start = lax.axis_index("dp") * own_rows
    shard_start = (
        lax.axis_index("dp") * lax.axis_size("vocab") + lax.axis_index("vocab")
    ) * shard_rows
    scale_factor = math.sqrt(D)
    local_ids = jnp.transpose(tokens) - shard_start
    columns = lax.broadcasted_iota(jnp.int32, (1, 1, shard_rows), 2)
    matches = local_ids[:, :, None] == columns
    onehot = matches.astype(jnp.bfloat16)
    found = jnp.einsum("sbv,vd->sbd", onehot, embed_table, preferred_element_type=jnp.float32)
    current = hidden
    partial_value = lax.psum_scatter(
        found.astype(jnp.bfloat16), "dp", scatter_dimension=1, tiled=True
    )
    summed = lax.psum(partial_value, "vocab").astype(jnp.float32)
    results = []
    for decode_step in range(STEPS):
        square_mean = jnp.mean(current * current, axis=-1, keepdims=True)
        normed = (current * lax.rsqrt(square_mean + epsilon_value) * norm_gain).astype(jnp.bfloat16)
        logits = project_rows(lax.all_gather(normed, "dp", axis=0, tiled=True), embed_table)
        capped = softcap_value * jnp.tanh(logits / softcap_value)
        exp_total = jnp.sum(jnp.exp(capped), axis=-1)
        target = jnp.sum(jnp.where(matches[decode_step], capped, 0.0), axis=-1)
        exp_total, target = lax.psum((exp_total, target), ("dp", "vocab"))
        exp_total = lax.dynamic_slice_in_dim(exp_total, own_start, own_rows, 0)
        target = lax.dynamic_slice_in_dim(target, own_start, own_rows, 0)
        results.append(target - jnp.log(exp_total))
        current = current + scale_factor * summed[decode_step]
    return (jnp.stack(results, axis=1), current)


def solution(mesh):
    return jax.shard_map(
        on_device,
        mesh=mesh,
        in_specs=(P("dp", None), P(), P(("dp", "vocab"), None), P()),
        out_specs=(P("dp", None), P("dp", None)),
        check_vma=False,
    )
```

profile of v0, /device:TPU:0, one launch (start us, length us, event | category | flops | bytes accessed | tf_op | source)
XLA Modules:
  0.0 184.3 jit_solution(427541426465696467)
XLA Ops:
  7.2 0.0 copy-start
  7.2 0.0 copy-start.3
  7.2 0.0 all-reduce.4.cloned.1.call-start
  7.2 0.8 subtract_bitcast_fusion
  8.1 1.1 copy-done
  9.2 1.5 convolution_convert_fusion
  10.7 0.0 all-reduce.4.cloned.1.call-update
  10.8 0.0 copy-done.3
  10.8 0.6 dynamic-slice
  12.0 0.7 iota_compare_fusion
  12.7 55.8 %all-reduce.4.cloned.1.call-done = bf16[3,16,4608]{2,1,0:T(8,128)(2,1)} async-done(((bf16[3,16,4608]{2,1,0:T(8,128)(2,1)}), bf16[3,16,4608]{2,1,0:T(8,128)(2,1)}) %all-reduce.4.cloned.1.call-update) | async-done | bytes 442384
  68.5 1.6 constant_dynamic-slice_fusion
  70.1 20.6 %psum.51 = bf16[3,2,4608]{2,1,0:T(2,128)(2,1)} all-reduce(bf16[3,2,4608]{2,1,0:T(2,128)(2,1)} %constant_dynamic-slice_fusion), channel_id=1, replica_groups=mesh['dp'=8,'vocab'=4] {'vocab'}, use_global_device_ids=true, to_apply=%region_6.7 | all-reduce | flops 27648 | bytes 110592 | tf_op jit(solution)/shard_map/psum | solution.py:39
  90.7 0.9 convert_element_type.18
  91.6 1.6 fusion.8
  93.2 0.2 multiply_reduce_fusion
  93.4 1.5 fusion.14
  94.9 9.6 %all-gather.2 = bf16[8,2,4608]{2,1,0:T(2,128)(2,1)} all-gather(bf16[1,2,4608]{2,1,0:T(2,128)(2,1)S(1)} %get-tuple-element.27), channel_id=1, replica_groups=mesh['dp'=8,'vocab'=4] {'dp'}, dimensions={0}, use_global_device_ids=true | all-gather | bytes 165888 | tf_op jit(solution)/shard_map/all_gather | solution.py:44
  104.5 1.6 reshape.41
  106.1 0.0 copy-start.2
  106.1 2.6 %fusion.2 = f32[16,384]{1,0:T(8,128)} fusion(bf16[16,4608]{1,0:T(8,128)(2,1)} %reshape.41, bf16[384,4608]{1,0:T(8,128)(2,1)S(1)} %copy-done), kind=kOutput, calls=%fused_computation.4 | convolution fusion | flops 56635392 | bytes 3710976 | tf_op jit(solution)/shard_map/dot_general | solution.py:17
  108.7 0.0 copy-done.2
  108.7 9.8 %all-gather.1 = bf16[8,2,4608]{2,1,0:T(2,128)(2,1)} all-gather(bf16[1,2,4608]{2,1,0:T(2,128)(2,1)S(1)} %copy-done.2), channel_id=1, replica_groups=mesh['dp'=8,'vocab'=4] {'dp'}, dimensions={0}, use_global_device_ids=true | all-gather | bytes 165888 | tf_op jit(solution)/shard_map/all_gather | solution.py:44
  118.5 1.6 reshape.39
  120.1 0.0 copy-start.1
  120.1 2.6 %fusion.4 = f32[16,384]{1,0:T(8,128)} fusion(bf16[16,4608]{1,0:T(8,128)(2,1)} %reshape.39, bf16[384,4608]{1,0:T(8,128)(2,1)S(1)} %copy-done), kind=kOutput, calls=%fused_computation.7 | convolution fusion | flops 56635392 | bytes 3710976 | tf_op jit(solution)/shard_map/dot_general | solution.py:17
  122.7 0.0 copy-done.1
  122.7 9.6 %all-gather = bf16[8,2,4608]{2,1,0:T(2,128)(2,1)} all-gather(bf16[1,2,4608]{2,1,0:T(2,128)(2,1)S(1)} %copy-done.1), channel_id=1, replica_groups=mesh['dp'=8,'vocab'=4] {'dp'}, dimensions={0}, use_global_device_ids=true | all-gather | bytes 165888 | tf_op jit(solution)/shard_map/all_gather | solution.py:44
  132.3 1.6 reshape.37
  133.9 2.8 %select_reduce_fusion.2 = (f32[16]{0:T(128)S(1)}, f32[16]{0:T(128)S(1)}, f32[16]{0:T(128)S(1)}, f32[16]{0:T(128)S(1)}, f32[16]{0:T(128)}, /*index=5*/f32[16]{0:T(128)}) fusion(pred[3,16,384]{2,1,0:T(8,128)(4,1)} %iota_compare_fusion, f32[16,384]{1,0:T(8,128)} %fusion.2, f32[16,384]{1,0:T(8,128)} %fusion.4, bf16[16,4608]{1,0:T(8,128)(2,1)} %reshape.37, ...), kind=kOutput, calls=%fused_computation.32 | convolution fusion | flops 56690592 | bytes 3754368 | tf_op jit(solution)/shard_map/dot_general | solution.py:17
  136.7 37.8 %all-reduce.1 = (f32[16]{0:T(128)}, f32[16]{0:T(128)}, f32[16]{0:T(128)}, f32[16]{0:T(128)}, f32[16]{0:T(128)}, /*index=5*/f32[16]{0:T(128)}) all-reduce(f32[16]{0:T(128)S(1)} %get-tuple-element.12, f32[16]{0:T(128)S(1)} %get-tuple-element.13, f32[16]{0:T(128)} %get-tuple-element.14, ...), channel_id=1, replica_groups=mesh['dp'=8,'vocab'=4] {'dp','vocab'}, use_global_device_ids=true, to_apply=%region_16.17 | all-reduce | flops 96 | bytes 768 | tf_op jit(solution)/shard_map/psum | solution.py:48
  174.5 0.7 subtract_bitcast_fusion.3
  175.3 0.7 subtract_bitcast_fusion.2
  176.0 0.8 subtract_bitcast_fusion.1
  176.8 0.7 copy.7
  (4 shorter events, 0.0 us)
Async XLA Ops:
  7.2 2.0 %copy-start = (bf16[384,4608]{1,0:T(8,128)(2,1)S(1)}, bf16[384,4608]{1,0:T(8,128)(2,1)}, u32[]{:S(2)}) copy-start(bf16[384,4608]{1,0:T(8,128)(2,1)} %param.6) | copy-start | bytes 10616836
  7.2 3.6 %copy-start.3 = (u32[32]{0:T(128)S(1)}, u32[32]{0:T(128)}, u32[]{:S(2)}) copy-start(u32[32]{0:T(128)} %constant.39) | copy-start | bytes 388
  7.2 61.3 %all-reduce.4.cloned.1.call-start = ((), (), s32[]{:S(2)}) async-start(), calls=%async_computation | async-start | bytes 884736
  106.1 2.6 %copy-start.2 = (bf16[1,2,4608]{2,1,0:T(2,128)(2,1)S(1)}, bf16[1,2,4608]{2,1,0:T(2,128)(2,1)}, u32[]{:S(2)}) copy-start(bf16[1,2,4608]{2,1,0:T(2,128)(2,1)} %get-tuple-element.26) | copy-start | bytes 55300
  120.1 2.6 %copy-start.1 = (bf16[1,2,4608]{2,1,0:T(2,128)(2,1)S(1)}, bf16[1,2,4608]{2,1,0:T(2,128)(2,1)}, u32[]{:S(2)}) copy-start(bf16[1,2,4608]{2,1,0:T(2,128)(2,1)} %get-tuple-element.28) | copy-start | bytes 55300
Sparse Core Ops, SparseCore 0:
  11.1 57.3 all-reduce.3
where the time goes:
time: 185 us; the launch traced here: 184 us
  blocking collectives  87.4 us (47%)
  waiting for transfers between devices  55.8 us (30%)
  between operations  14.8 us (8%)
  matrix products  9.53 us (5%)
  local copies, waits for them, and re-layouts  8.82 us (5%)
  other arithmetic  7.92 us (4%)
    unnamed x2, waiting for transfers between devices  55.8 us
    psum x1, blocking collectives, on_device(): exp_total, target = lax.psum((exp_total, target), ('dp', 'vocab'))  37.8 us
    all_gather x3, blocking collectives, on_device(): lax.all_gather(normed, 'dp', axis=0, tiled=True)  29 us
    psum x1, blocking collectives, on_device(): summed = lax.psum(partial_value, 'vocab').astype(jnp.float32)  20.6 us
    unnamed x14, local copies, waits for them, and re-layouts  8.82 us
    dot_general x3, matrix products, project_rows(): lax.dot_general(normed, embed_table, (((1,), (1,)), ((), ())), preferred_...  7.99 us
  transfers between devices with their start and end apart: 1, of which 1 were waited for; matrix products, arithmetic and copies ran while one was open for 1% of the time, Pallas kernels for 0%

commit v1 on v0

v1 whole, which is shorter than its diff:
```python
import functools
import math

import jax
import jax.numpy as jnp
from jax import lax
from jax.experimental import pallas as pl
from jax.experimental.pallas import tpu as pltpu
from jax.sharding import PartitionSpec as P

epsilon_value = 1e-06
softcap_value = 30.0
STEPS = 3
CHUNKS = 4


def each(low, high, body):
    if high - low <= 8:
        for k in range(low, high):
            body(k)
    else:
        pl.loop(low, high)(body)


def folded(low, high, body, init):
    if high - low <= 8:
        for k in range(low, high):
            init = body(k, init)
        return init
    return lax.fori_loop(low, high, body, init)


def contract(a, b):
    return lax.dot_general(a, b, (((1,), (1,)), ((), ())), preferred_element_type=jnp.float32)


def kernel(
    n_dp, n_vocab,
    hidden, gain, tokens, table, logp, final,
    tab, rows, found, found2, got_a, got_a2, part, part2, got_b, got_b2,
    state0, state1, wide0, wide1, sums, got_d,
    tab_sem, s0, r0, sa, ra, sa2, ra2, sb, rb, sb2, rb2, sc, rc, sd, rd,
):
    dp, voc = lax.axis_index("dp"), lax.axis_index("vocab")
    own, width = hidden.shape
    shard = table.shape[0]
    batch = tokens.shape[0]
    scale = math.sqrt(width)
    cut = width // CHUNKS

    loads = [
        pltpu.make_async_copy(
            table.at[:, pl.ds(i * cut, cut)], tab.at[:, pl.ds(i * cut, cut)], tab_sem.at[i]
        )
        for i in range(CHUNKS)
    ]
    for load in loads:
        load.start()

    barrier = pltpu.get_barrier_semaphore()

    def greet(k):
        pl.semaphore_signal(
            barrier, inc=1,
            device_id={"dp": lax.rem(dp + k // n_vocab, n_dp), "vocab": lax.rem(voc + k % n_vocab, n_vocab)},
            device_id_type=pl.DeviceIdType.MESH,
        )

    pl.loop(1, n_dp * n_vocab)(greet)

    def remote(src, dst, send, recv, target):
        return pltpu.make_async_remote_copy(
            src_ref=src, dst_ref=dst, send_sem=send, recv_sem=recv,
            device_id=target, device_id_type=pl.DeviceIdType.MESH,
        )

    def to_dp(k):
        return lax.rem(dp + k, n_dp)

    def from_dp(k):
        return lax.rem(dp + n_dp - k, n_dp)

    def normed_of(current):
        square_mean = jnp.mean(current * current, axis=-1, keepdims=True)
        return (current * lax.rsqrt(square_mean + epsilon_value) * gain[...]).astype(jnp.bfloat16)

    state0[dp] = normed_of(hidden[...])
    start_row = (dp * n_vocab + voc) * shard
    columns = lax.broadcasted_iota(jnp.int32, (batch, shard), 1)
    ids = tokens[...] - start_row
    matches = [columns == ids[:, s : s + 1] for s in range(STEPS)]
    onehot = jnp.concatenate(
        [jnp.where(m, 1.0, 0.0).astype(jnp.bfloat16) for m in matches], axis=0
    )

    pl.semaphore_wait(barrier, n_dp * n_vocab - 1)

    def copy0(k, slot):
        return remote(state0.at[dp], state0.at[slot], s0.at[k], r0.at[k], {"dp": to_dp(k)})

    each(1, n_dp, lambda k: copy0(k, dp).start())

    for i in range(CHUNKS):
        loads[i].wait()
        at = slice(i * cut, (i + 1) * cut)
        rows[:, at] = jnp.dot(onehot, tab[:, at], preferred_element_type=jnp.float32)
    for d in range(n_dp):
        for s in range(STEPS):
            piece = rows[s * batch + d * own : s * batch + (d + 1) * own, :].astype(jnp.bfloat16)
            if s < STEPS - 1:
                found[d, s * own : (s + 1) * own, :] = piece
            else:
                found2[d] = piece

    def copy_a(k):
        return remote(found.at[to_dp(k)], got_a.at[k], sa.at[k], ra.at[k], {"dp": to_dp(k)})

    def copy_a2(k):
        return remote(found2.at[to_dp(k)], got_a2.at[k], sa2.at[k], ra2.at[k], {"dp": to_dp(k)})

    each(1, n_dp, lambda k: copy_a(k).start())
    each(1, n_dp, lambda k: copy_a2(k).start())

    lane = lax.broadcasted_iota(jnp.int32, (batch, sums.shape[2]), 1)

    def reduced(logits, s):
        capped = softcap_value * jnp.tanh(logits / softcap_value)
        exp_total = jnp.sum(jnp.exp(capped), axis=-1, keepdims=True)
        target = jnp.sum(jnp.where(matches[s], capped, 0.0), axis=-1, keepdims=True)
        return jnp.where(lane == s, exp_total, 0.0) + jnp.where(lane == STEPS + s, target, 0.0)

    each(1, n_dp, lambda k: copy0(k, from_dp(k)).wait_recv())
    for d in range(n_dp):
        wide0[d * own : (d + 1) * own, :] = state0[d].astype(jnp.float32)
    partial = reduced(contract(wide0[...].astype(jnp.bfloat16), tab[...]), 0)

    def add_a(k, acc):
        copy_a(k).wait_recv()
        return acc + got_a[k]

    part[...] = folded(1, n_dp, add_a, found[dp])

    def copy_b(k):
        return remote(part, got_b.at[k], sb.at[k], rb.at[k], {"vocab": lax.rem(voc + k, n_vocab)})

    def copy_b2(k):
        return remote(part2, got_b2.at[k], sb2.at[k], rb2.at[k], {"vocab": lax.rem(voc + k, n_vocab)})

    each(1, n_vocab, lambda k: copy_b(k).start())

    def add_a2(k, acc):
        copy_a2(k).wait_recv()
        return acc + got_a2[k]

    part2[...] = folded(1, n_dp, add_a2, found2[dp])
    each(1, n_vocab, lambda k: copy_b2(k).start())

    def add_b(k, acc):
        copy_b(k).wait_recv()
        return acc + got_b[k]

    looked = folded(1, n_vocab, add_b, part[...]).astype(jnp.float32)
    current = hidden[...]
    for s in range(STEPS - 1):
        current = current + scale * looked[s * own : (s + 1) * own, :]
        state1[dp, s * own : (s + 1) * own, :] = normed_of(current)

    def copy_c(k, slot):
        return remote(state1.at[dp], state1.at[slot], sc.at[k], rc.at[k], {"dp": to_dp(k)})

    each(1, n_dp, lambda k: copy_c(k, dp).start())

    def add_b2(k, acc):
        copy_b2(k).wait_recv()
        return acc + got_b2[k]

    final[...] = current + scale * folded(1, n_vocab, add_b2, part2[...]).astype(jnp.float32)

    each(1, n_dp, lambda k: copy_c(k, from_dp(k)).wait_recv())
    for d in range(n_dp):
        for s in range(STEPS - 1):
            wide1[s * batch + d * own : s * batch + (d + 1) * own, :] = state1[
                d, s * own : (s + 1) * own, :
            ].astype(jnp.float32)
    logits = contract(wide1[...].astype(jnp.bfloat16), tab[...])
    for s in range(1, STEPS):
        partial = partial + reduced(logits[(s - 1) * batch : s * batch], s)
    for d in range(n_dp):
        sums[d] = partial[d * own : (d + 1) * own, :]

    def copy_d(k):
        d = lax.rem(dp + k // n_vocab, n_dp)
        v = lax.rem(voc + k % n_vocab, n_vocab)
        return remote(sums.at[d], got_d.at[k], sd.at[k], rd.at[k], {"dp": d, "vocab": v})

    pl.loop(1, n_dp * n_vocab)(lambda k: copy_d(k).start())
    got_d[0] = sums[dp]

    each(1, n_dp, lambda k: copy0(k, dp).wait_send())
    each(1, n_dp, lambda k: copy_a(k).wait_send())
    each(1, n_dp, lambda k: copy_a2(k).wait_send())
    each(1, n_vocab, lambda k: copy_b(k).wait_send())
    each(1, n_vocab, lambda k: copy_b2(k).wait_send())
    each(1, n_dp, lambda k: copy_c(k, dp).wait_send())
    pl.loop(1, n_dp * n_vocab)(lambda k: copy_d(k).wait_recv())
    total = jnp.sum(got_d[...], axis=0)
    logp[...] = total[:, STEPS : 2 * STEPS] - jnp.log(total[:, :STEPS])
    pl.loop(1, n_dp * n_vocab)(lambda k: copy_d(k).wait_send())


def on_device(n_dp, n_vocab, hidden, norm_gain, embed_table, tokens):
    own, width = hidden.shape
    shard = embed_table.shape[0]
    batch = tokens.shape[0]
    early = (STEPS - 1) * own
    bf16, f32 = jnp.bfloat16, jnp.float32
    vmem = pl.BlockSpec(memory_space=pltpu.VMEM)
    dma = pltpu.SemaphoreType.DMA
    everyone = n_dp * n_vocab
    return pl.pallas_call(
        functools.partial(kernel, n_dp, n_vocab),
        out_shape=(
            jax.ShapeDtypeStruct((own, STEPS), f32),
            jax.ShapeDtypeStruct((own, width), f32),
        ),
        in_specs=[vmem, vmem, vmem, pl.BlockSpec(memory_space=pl.ANY)],
        out_specs=(vmem, vmem),
        scratch_shapes=[
            pltpu.VMEM((shard, width), bf16),
            pltpu.VMEM((STEPS * batch, width), f32),
            pltpu.VMEM((n_dp, early, width), bf16),
            pltpu.VMEM((n_dp, own, width), bf16),
            pltpu.VMEM((n_dp, early, width), bf16),
            pltpu.VMEM((n_dp, own, width), bf16),
            pltpu.VMEM((early, width), bf16),
            pltpu.VMEM((own, width), bf16),
            pltpu.VMEM((n_vocab, early, width), bf16),
            pltpu.VMEM((n_vocab, own, width), bf16),
            pltpu.VMEM((n_dp, own, width), bf16),
            pltpu.VMEM((n_dp, early, width), bf16),
            pltpu.VMEM((batch, width), f32),
            pltpu.VMEM((early * n_dp, width), f32),
            pltpu.VMEM((n_dp, own, 128), f32),
            pltpu.VMEM((everyone, own, 128), f32),
            dma((CHUNKS,)),
            dma((n_dp,)), dma((n_dp,)),
            dma((n_dp,)), dma((n_dp,)),
            dma((n_dp,)), dma((n_dp,)),
            dma((n_vocab,)), dma((n_vocab,)),
            dma((n_vocab,)), dma((n_vocab,)),
            dma((n_dp,)), dma((n_dp,)),
            dma((everyone,)), dma((everyone,)),
        ],
        compiler_params=pltpu.CompilerParams(
            collective_id=0, has_side_effects=True, vmem_limit_bytes=48 * 1024 * 1024
        ),
    )(hidden, norm_gain.reshape(1, width), tokens, embed_table)


def solution(mesh):
    return jax.shard_map(
        functools.partial(on_device, mesh.shape["dp"], mesh.shape["vocab"]),
        mesh=mesh,
        in_specs=(P("dp", None), P(), P(("dp", "vocab"), None), P()),
        out_specs=(P("dp", None), P("dp", None)),
        check_vma=False,
    )
```

time: 185 us -> 39.1 us (0.21)
  blocking collectives: 87.4 us -> 0 us
  waiting for transfers between devices: 55.8 us -> 0 us
  Pallas kernels: 0 us -> 32.7 us
  between operations: 14.8 us -> 0.65 us
  matrix products: 9.53 us -> 0 us
  other arithmetic: 7.92 us -> 0 us
  local copies, waits for them, and re-layouts: 8.82 us -> 5.44 us
    psum x2 -> x0, blocking collectives: 58.4 us -> none  [the longest x1 37.8 us: on_device(): exp_total, target = lax.psum((exp_total, target), ('dp', 'vocab'))]
    unnamed x2 -> x0, waiting for transfers between devices: 55.8 us -> none
    pallas_call x0 -> x1, Pallas kernels: none -> 32.7 us  [on_device(): pl.pallas_call(functools.partial(kernel, n_dp, n_vocab), out_shape=(jax.S...]
    all_gather x3 -> x0, blocking collectives: 29 us -> none  [on_device(): lax.all_gather(normed, 'dp', axis=0, tiled=True)]
    dot_general x4 -> x0, matrix products: 9.53 us -> none  [the longest x3 7.99 us: project_rows(): lax.dot_general(normed, embed_table, (((1,), (1,)), ((), ())), preferred_...]
    unnamed x14 -> x7, local copies, waits for them, and re-layouts: 8.82 us -> 4.7 us
    another operation x4 -> x0, other arithmetic: 2.26 us -> none  [on_device(): return (jnp.stack(results, axis=1), current)]
  transfers between devices with their start and end apart: 1 -> 0, of which waited for: 1 -> 0; matrix products, arithmetic and copies ran while one was open for 1% -> 0% of each run, Pallas kernels for 0% -> 0%
where the time goes in v1:
time: 39.1 us; the launch traced here: 38.8 us
  Pallas kernels  32.7 us (84%)
  local copies, waits for them, and re-layouts  5.44 us (14%)
  between operations  0.65 us (2%)
    pallas_call x1, Pallas kernels, on_device(): pl.pallas_call(functools.partial(kernel, n_dp, n_vocab), out_shape=(jax.S...  32.7 us
    unnamed x7, local copies, waits for them, and re-layouts  4.7 us

profile of v1, /device:TPU:0, one launch (start us, length us, event | category | flops | bytes accessed | tf_op | source)
XLA Modules:
  0.0 38.8 jit_solution(3945674310431709226)
XLA Ops:
  0.6 0.8 %copy.6.tokens = s32[16,3]{1,0:T(8,128)S(1)} copy(s32[16,3]{0,1:T(4,128)} %param.7) | data formatting | bytes 384 | tf_op args[3]
  1.4 0.7 %reshape.7.gain = f32[1,4608]{1,0:T(1,128)S(1)} reshape(f32[4608]{0:T(1024)} %param.5) | data formatting | bytes 36864 | tf_op jit(solution)/shard_map/reshape | solution.py:257
  2.1 0.0 copy-start
  2.1 2.0 %copy-done = bf16[384,4608]{1,0:T(8,128)(2,1)S(1)} copy-done((bf16[384,4608]{1,0:T(8,128)(2,1)S(1)}, bf16[384,4608]{1,0:T(8,128)(2,1)}, u32[]{:S(2)}) %copy-start) | copy-done | bytes 3538968
  4.1 0.0 copy-start.1
  4.1 0.8 %copy-done.1 = f32[2,4608]{1,0:T(2,128)S(1)} copy-done((f32[2,4608]{1,0:T(2,128)S(1)}, f32[2,4608]{1,0:T(2,128)}, u32[]{:S(2)}) %copy-start.1) | copy-done | bytes 36888
  4.9 32.7 %shard_map.59 = (f32[2,3]{1,0:T(2,128)S(1)}, f32[2,4608]{1,0:T(2,128)S(1)}) custom-call(f32[2,4608]{1,0:T(2,128)S(1)} %copy-done.1, f32[1,4608]{1,0:T(1,128)S(1)} %reshape.7.gain, s32[16,3]{1,0:T(8,128)S(1)} %copy.6.tokens, bf16[384,4608]{1,0:T(8,128)(2,1)S(1)} %copy-done), custom_call_target="tpu_custom_call" | custom-call | tf_op jit(solution)/shard_map/pallas_call | solution.py:220
  37.6 0.6 %copy.9 = f32[2,3]{1,0:T(2,128)} copy(f32[2,3]{1,0:T(2,128)S(1)} %get-tuple-element.4) | data formatting | bytes 48
  38.1 0.6 %copy.10 = f32[2,4608]{1,0:T(2,128)} copy(f32[2,4608]{1,0:T(2,128)S(1)} %get-tuple-element.5) | data formatting | bytes 73728
Async XLA Ops:
  2.1 2.0 %copy-start = (bf16[384,4608]{1,0:T(8,128)(2,1)S(1)}, bf16[384,4608]{1,0:T(8,128)(2,1)}, u32[]{:S(2)}) copy-start(bf16[384,4608]{1,0:T(8,128)(2,1)} %table.1) | copy-start | bytes 10616836
  4.1 0.8 %copy-start.1 = (f32[2,4608]{1,0:T(2,128)S(1)}, f32[2,4608]{1,0:T(2,128)}, u32[]{:S(2)}) copy-start(f32[2,4608]{1,0:T(2,128)} %hidden.1) | copy-start | bytes 110596

commit v2 on v1

v2 whole, which is shorter than its diff:
```python
import functools
import math

import jax
import jax.numpy as jnp
from jax import lax
from jax.experimental import pallas as pl
from jax.experimental.pallas import tpu as pltpu
from jax.sharding import PartitionSpec as P

epsilon_value = 1e-06
softcap_value = 30.0
STEPS = 3
CHUNKS = 4


def each(low, high, body):
    if high - low <= 8:
        for k in range(low, high):
            body(k)
    else:
        pl.loop(low, high)(body)


def folded(low, high, body, init):
    if high - low <= 8:
        for k in range(low, high):
            init = body(k, init)
        return init
    return lax.fori_loop(low, high, body, init)


def contract(a, b):
    return lax.dot_general(a, b, (((1,), (1,)), ((), ())), preferred_element_type=jnp.float32)


def kernel(
    n_dp, n_vocab,
    hidden_in, gain_in, tokens, table, logp, final,
    hidden, gain, tab, found, found2, got_a, got_a2, part, part2, got_b, got_b2,
    hidden_all, looked, base, wide, sums, got_d,
    in_sem, tab_sem, sh, rh, sa, ra, sa2, ra2, sb, rb, sb2, rb2, sc, rc, sd, rd,
):
    dp, voc = lax.axis_index("dp"), lax.axis_index("vocab")
    own, width = hidden.shape
    shard = table.shape[0]
    batch = tokens.shape[1]
    scale = math.sqrt(width)
    cut = width // CHUNKS
    early = (STEPS - 1) * own

    barrier = pltpu.get_barrier_semaphore()

    def greet(k):
        pl.semaphore_signal(
            barrier, inc=1,
            device_id={"dp": lax.rem(dp + k // n_vocab, n_dp), "vocab": lax.rem(voc + k % n_vocab, n_vocab)},
            device_id_type=pl.DeviceIdType.MESH,
        )

    pl.loop(1, n_dp * n_vocab)(greet)

    loads = [
        pltpu.make_async_copy(
            table.at[:, pl.ds(i * cut, cut)], tab.at[:, pl.ds(i * cut, cut)], tab_sem.at[i]
        )
        for i in range(CHUNKS)
    ]
    fetches = [
        pltpu.make_async_copy(hidden_in, hidden, in_sem.at[0]),
        pltpu.make_async_copy(gain_in, gain.at[0], in_sem.at[1]),
    ]
    for copy in loads + fetches:
        copy.start()

    def remote(src, dst, send, recv, target):
        return pltpu.make_async_remote_copy(
            src_ref=src, dst_ref=dst, send_sem=send, recv_sem=recv,
            device_id=target, device_id_type=pl.DeviceIdType.MESH,
        )

    def to_dp(k):
        return lax.rem(dp + k, n_dp)

    def from_dp(k):
        return lax.rem(dp + n_dp - k, n_dp)

    start_row = (dp * n_vocab + voc) * shard
    columns = lax.broadcasted_iota(jnp.int32, (batch, shard), 1)
    diagonal = lax.broadcasted_iota(jnp.int32, (batch, batch), 0) == lax.broadcasted_iota(
        jnp.int32, (batch, batch), 1
    )
    local = (tokens[...] - start_row).astype(jnp.float32)
    matches = []
    for s in range(STEPS):
        ids = jnp.sum(jnp.where(diagonal, local[s : s + 1, :], 0.0), axis=1, keepdims=True)
        matches.append(columns == ids.astype(jnp.int32))
    onehot = jnp.concatenate(
        [jnp.where(m, 1.0, 0.0).astype(jnp.bfloat16) for m in matches], axis=0
    )

    for i in range(CHUNKS):
        loads[i].wait()
        at = slice(i * cut, (i + 1) * cut)
        rows = jnp.dot(onehot, tab[:, at], preferred_element_type=jnp.float32)
        for d in range(n_dp):
            for s in range(STEPS):
                piece = rows[s * batch + d * own : s * batch + (d + 1) * own, :].astype(jnp.bfloat16)
                if s < STEPS - 1:
                    found[i, d, s * own : (s + 1) * own, :] = piece
                else:
                    found2[d, :, at] = piece
    for copy in fetches:
        copy.wait()

    pl.semaphore_wait(barrier, n_dp * n_vocab - 1)

    def copy_a(i, k):
        return remote(
            found.at[i, to_dp(k)], got_a.at[i, k], sa.at[i, k], ra.at[i, k], {"dp": to_dp(k)}
        )

    def copy_h(k, slot):
        return remote(hidden, hidden_all.at[slot], sh.at[k], rh.at[k], {"dp": to_dp(k)})

    def copy_a2(k):
        return remote(found2.at[to_dp(k)], got_a2.at[k], sa2.at[k], ra2.at[k], {"dp": to_dp(k)})

    for i in range(CHUNKS):
        each(1, n_dp, lambda k: copy_a(i, k).start())
    each(1, n_dp, lambda k: copy_h(k, dp).start())
    each(1, n_dp, lambda k: copy_a2(k).start())
    hidden_all[dp] = hidden[...]

    lane = lax.broadcasted_iota(jnp.int32, (batch, sums.shape[2]), 1)

    def reduced(logits, s):
        capped = softcap_value * jnp.tanh(logits / softcap_value)
        exp_total = jnp.sum(jnp.exp(capped), axis=-1, keepdims=True)
        target = jnp.sum(jnp.where(matches[s], capped, 0.0), axis=-1, keepdims=True)
        return jnp.where(lane == s, exp_total, 0.0) + jnp.where(lane == STEPS + s, target, 0.0)

    def normed(current, squares):
        return (current * lax.rsqrt(squares / width + epsilon_value) * gain[...]).astype(jnp.bfloat16)

    def copy_b(i, k):
        return remote(
            part.at[i], got_b.at[i, k], sb.at[i, k], rb.at[i, k], {"vocab": lax.rem(voc + k, n_vocab)}
        )

    for i in range(CHUNKS):

        def add_a(k, acc):
            copy_a(i, k).wait_recv()
            return acc + got_a[i, k]

        part[i] = folded(1, n_dp, add_a, found[i, dp])
        each(1, n_vocab, lambda k: copy_b(i, k).start())

    def copy_c(i, k, slot):
        return remote(looked.at[i, dp], looked.at[i, slot], sc.at[i, k], rc.at[i, k], {"dp": to_dp(k)})

    for i in range(CHUNKS):

        def add_b(k, acc):
            copy_b(i, k).wait_recv()
            return acc + got_b[i, k]

        looked[i, dp] = folded(1, n_vocab, add_b, part[i])
        each(1, n_dp, lambda k: copy_c(i, k, dp).start())

    def copy_b2(k):
        return remote(part2, got_b2.at[k], sb2.at[k], rb2.at[k], {"vocab": lax.rem(voc + k, n_vocab)})

    def add_a2(k, acc):
        copy_a2(k).wait_recv()
        return acc + got_a2[k]

    part2[...] = folded(1, n_dp, add_a2, found2[dp])
    each(1, n_vocab, lambda k: copy_b2(k).start())

    each(1, n_dp, lambda k: copy_h(k, from_dp(k)).wait_recv())
    for d in range(n_dp):
        base[d * own : (d + 1) * own, :] = hidden_all[d]
    first = base[...]
    partial = reduced(
        contract(normed(first, jnp.sum(first * first, axis=-1, keepdims=True)), tab[...]), 0
    )

    squares = [jnp.zeros((batch, 1), jnp.float32) for s in range(STEPS - 1)]
    for i in range(CHUNKS):
        at = slice(i * cut, (i + 1) * cut)
        each(1, n_dp, lambda k: copy_c(i, k, from_dp(k)).wait_recv())
        for d in range(n_dp):
            for s in range(STEPS - 1):
                wide[s * batch + d * own : s * batch + (d + 1) * own, at] = looked[
                    i, d, s * own : (s + 1) * own, :
                ].astype(jnp.float32)
        current = base[:, at]
        for s in range(STEPS - 1):
            current = current + scale * wide[s * batch : (s + 1) * batch, at]
            squares[s] += jnp.sum(current * current, axis=-1, keepdims=True)
            wide[s * batch : (s + 1) * batch, at] = current
    logits = contract(normed(wide[...], jnp.concatenate(squares, axis=0)), tab[...])
    for s in range(1, STEPS):
        partial = partial + reduced(logits[(s - 1) * batch : s * batch], s)
    for d in range(n_dp):
        sums[d] = partial[d * own : (d + 1) * own, :]

    def copy_d(k):
        d = lax.rem(dp + k // n_vocab, n_dp)
        v = lax.rem(voc + k % n_vocab, n_vocab)
        return remote(sums.at[d], got_d.at[k], sd.at[k], rd.at[k], {"dp": d, "vocab": v})

    pl.loop(1, n_dp * n_vocab)(lambda k: copy_d(k).start())
    got_d[0] = sums[dp]

    def add_b2(k, acc):
        copy_b2(k).wait_recv()
        return acc + got_b2[k]

    last = folded(1, n_vocab, add_b2, part2[...])
    for i in range(CHUNKS):
        at = slice(i * cut, (i + 1) * cut)
        current = hidden[:, at]
        mine = looked[i, dp].astype(jnp.float32)
        for s in range(STEPS - 1):
            current = current + scale * mine[s * own : (s + 1) * own, :]
        final[:, at] = current + scale * last[:, at].astype(jnp.float32)

    for i in range(CHUNKS):
        each(1, n_dp, lambda k: copy_a(i, k).wait_send())
        each(1, n_vocab, lambda k: copy_b(i, k).wait_send())
        each(1, n_dp, lambda k: copy_c(i, k, dp).wait_send())
    each(1, n_dp, lambda k: copy_h(k, dp).wait_send())
    each(1, n_dp, lambda k: copy_a2(k).wait_send())
    each(1, n_vocab, lambda k: copy_b2(k).wait_send())
    pl.loop(1, n_dp * n_vocab)(lambda k: copy_d(k).wait_recv())
    total = jnp.sum(got_d[...], axis=0)
    logp[...] = total[:, STEPS : 2 * STEPS] - jnp.log(total[:, :STEPS])
    pl.loop(1, n_dp * n_vocab)(lambda k: copy_d(k).wait_send())


def on_device(n_dp, n_vocab, hidden, norm_gain, embed_table, tokens):
    own, width = hidden.shape
    shard = embed_table.shape[0]
    batch = tokens.shape[0]
    early = (STEPS - 1) * own
    cut = width // CHUNKS
    bf16, f32 = jnp.bfloat16, jnp.float32
    vmem = pl.BlockSpec(memory_space=pltpu.VMEM)
    outside = pl.BlockSpec(memory_space=pl.ANY)
    dma = pltpu.SemaphoreType.DMA
    everyone = n_dp * n_vocab
    return pl.pallas_call(
        functools.partial(kernel, n_dp, n_vocab),
        out_shape=(
            jax.ShapeDtypeStruct((own, STEPS), f32),
            jax.ShapeDtypeStruct((own, width), f32),
        ),
        in_specs=[outside, outside, vmem, outside],
        out_specs=(vmem, vmem),
        scratch_shapes=[
            pltpu.VMEM((own, width), f32),
            pltpu.VMEM((1, width), f32),
            pltpu.VMEM((shard, width), bf16),
            pltpu.VMEM((CHUNKS, n_dp, early, cut), bf16),
            pltpu.VMEM((n_dp, own, width), bf16),
            pltpu.VMEM((CHUNKS, n_dp, early, cut), bf16),
            pltpu.VMEM((n_dp, own, width), bf16),
            pltpu.VMEM((CHUNKS, early, cut), bf16),
            pltpu.VMEM((own, width), bf16),
            pltpu.VMEM((CHUNKS, n_vocab, early, cut), bf16),
            pltpu.VMEM((n_vocab, own, width), bf16),
            pltpu.VMEM((n_dp, own, width), f32),
            pltpu.VMEM((CHUNKS, n_dp, early, cut), bf16),
            pltpu.VMEM((batch, width), f32),
            pltpu.VMEM((early * n_dp, width), f32),
            pltpu.VMEM((n_dp, own, 128), f32),
            pltpu.VMEM((everyone, own, 128), f32),
            dma((2,)), dma((CHUNKS,)),
            dma((n_dp,)), dma((n_dp,)),
            dma((CHUNKS, n_dp)), dma((CHUNKS, n_dp)),
            dma((n_dp,)), dma((n_dp,)),
            dma((CHUNKS, n_vocab)), dma((CHUNKS, n_vocab)),
            dma((n_vocab,)), dma((n_vocab,)),
            dma((CHUNKS, n_dp)), dma((CHUNKS, n_dp)),
            dma((everyone,)), dma((everyone,)),
        ],
        compiler_params=pltpu.CompilerParams(
            collective_id=0, has_side_effects=True, vmem_limit_bytes=60 * 1024 * 1024
        ),
    )(hidden, norm_gain, jnp.transpose(tokens), embed_table)


def solution(mesh):
    return jax.shard_map(
        functools.partial(on_device, mesh.shape["dp"], mesh.shape["vocab"]),
        mesh=mesh,
        in_specs=(P("dp", None), P(), P(("dp", "vocab"), None), P()),
        out_specs=(P("dp", None), P("dp", None)),
        check_vma=False,
    )
```

time: 39.1 us -> 33.4 us (0.85)
  local copies, waits for them, and re-layouts: 5.44 us -> 2.58 us
  Pallas kernels: 32.7 us -> 29.9 us
    pallas_call x1, Pallas kernels: 32.7 us -> 29.9 us  [on_device(): pl.pallas_call(functools.partial(kernel, n_dp, n_vocab), out_shape=(jax.S...]
    unnamed x7 -> x2, local copies, waits for them, and re-layouts: 4.7 us -> 2.58 us
    reshape x1 -> x0, local copies, waits for them, and re-layouts: 0.74 us -> none  [on_device(): norm_gain.reshape(1, width)]
where the time goes in v2:
time: 33.4 us; the launch traced here: 33.2 us
  Pallas kernels  29.9 us (90%)
  local copies, waits for them, and re-layouts  2.58 us (8%)
  between operations  0.64 us (2%)
    pallas_call x1, Pallas kernels, on_device(): pl.pallas_call(functools.partial(kernel, n_dp, n_vocab), out_shape=(jax.S...  29.9 us
    unnamed x2, local copies, waits for them, and re-layouts  2.58 us

profile of v2, /device:TPU:0, one launch (start us, length us, event | category | flops | bytes accessed | tf_op | source)
XLA Modules:
  0.0 33.2 jit_solution(9420573631197869025)
XLA Ops:
  0.6 29.9 %shard_map.59 = (f32[2,3]{1,0:T(2,128)}, f32[2,4608]{1,0:T(2,128)}) custom-call(f32[2,4608]{1,0:T(2,128)} %hidden_in.1, f32[4608]{0:T(1024)} %gain_in.1, s32[3,16]{1,0:T(4,128)} %bitcast.1, bf16[384,4608]{1,0:T(8,128)(2,1)} %table.1), custom_call_target="tpu_custom_call" | custom-call | tf_op jit(solution)/shard_map/pallas_call | solution.py:255
  30.6 1.2 %copy.8 = f32[2,3]{1,0:T(2,128)} copy(f32[2,3]{1,0:T(2,128)} %get-tuple-element.4) | data formatting | bytes 48
  31.8 1.4 %copy.9 = f32[2,4608]{1,0:T(2,128)} copy(f32[2,4608]{1,0:T(2,128)} %get-tuple-element.5) | data formatting | bytes 73728
